TPU v7x, 32 devices: a whole 2x2x4 slice. The times are simulated.
32 devices in a mesh: vert: 8 (over z, y), col: 4 (over x, core).
Axes of the slice: x: 2, y: 2, z: 4, core: 2. Of those that a mesh axis runs over, the one named last changes fastest.
Arguments:
- coeffs: bfloat16 [64, 400], P(('vert', 'col')), may hold values from -6 to 6
- shape_basis: bfloat16 [400, 3, 656], P('col', None, 'vert'), may hold values from -0.3125 to 0.3125
- template: float32 [3, 656], P(None, 'vert'), may hold values from -6 to 6
- regressor: float32 [55, 656], P(None, 'vert'), may hold values from -0.5 to 0.5
- quaternions: float32 [64, 4, 55], P(('vert', 'col')), may hold values from -1.5 to 1.5, as said below
- translation: float32 [64, 3], P(('vert', 'col')), may hold values from -6 to 6
- parents: int32 [55], replicated, may hold values from 0 to 53, as said below
- skin_index: int32 [656, 4], P('vert'), may hold values from 0 to 54, all different within a row
- skin_raw: float32 [656, 4], P('vert'), may hold values from 0.1 to 1
Outputs:
- posed_vertices: bfloat16 [64, 3, 656], P(('vert', 'col'))
Inputs may be any that keep to these rules, and one draw needn't show every extreme that they name: parents[0] = 0 and parents[j] < j for j >= 1. `skin_index`: the four joints of a vertex differ. `quaternions`: component 0 lies in [0.5, 1.5].
All inputs are finite; a program needn't handle non-finite values.
Results may differ from a plain program's by a relative error of at most 0.0024.
Values may be sent and summed in bfloat16 or wider, within the bound.
A program may use at most 64 MiB of HBM per device.

v0:
```python
import jax
import jax.numpy as jnp
from jax import lax
from jax.sharding import PartitionSpec as P


def rotations(quaternions):
    quat_w = jnp.transpose(quaternions[:, 0])
    quat_x = jnp.transpose(quaternions[:, 1])
    quat_y = jnp.transpose(quaternions[:, 2])
    quat_z = jnp.transpose(quaternions[:, 3])
    scale_two = 2.0 / (quat_w * quat_w + quat_x * quat_x + quat_y * quat_y + quat_z * quat_z)
    matrix_rows = [
        [
            1.0 - scale_two * (quat_y * quat_y + quat_z * quat_z),
            scale_two * (quat_x * quat_y - quat_w * quat_z),
            scale_two * (quat_x * quat_z + quat_w * quat_y),
        ],
        [
            scale_two * (quat_x * quat_y + quat_w * quat_z),
            1.0 - scale_two * (quat_x * quat_x + quat_z * quat_z),
            scale_two * (quat_y * quat_z - quat_w * quat_x),
        ],
        [
            scale_two * (quat_x * quat_z - quat_w * quat_y),
            scale_two * (quat_y * quat_z + quat_w * quat_x),
            1.0 - scale_two * (quat_x * quat_x + quat_y * quat_y),
        ],
    ]
    return jnp.stack([jnp.stack(entry, axis=1) for entry in matrix_rows], axis=1)


def kinematics(joints, quaternions, translation, parents):
    joint_total = quaternions.shape[2]
    local_rots = rotations(quaternions)
    places = jnp.transpose(joints, (2, 1, 0))
    glob_rot = jnp.zeros_like(local_rots).at[0].set(local_rots[0])
    glob_pos = jnp.zeros_like(places).at[0].set(places[0] + jnp.transpose(translation))

    def compose(joint, state_pair):
        rot_now, pos_now = state_pair
        parent = lax.dynamic_index_in_dim(parents, joint, 0, keepdims=False)
        parent_rot = lax.dynamic_index_in_dim(rot_now, parent, 0, keepdims=False)
        parent_pos = lax.dynamic_index_in_dim(pos_now, parent, 0, keepdims=False)
        local_rot = lax.dynamic_index_in_dim(local_rots, joint, 0, keepdims=False)
        offset = lax.dynamic_index_in_dim(
            places, joint, 0, keepdims=False
        ) - lax.dynamic_index_in_dim(places, parent, 0, keepdims=False)
        new_rot = jnp.einsum("amc,mbc->abc", parent_rot, local_rot, precision=lax.Precision.HIGHEST)
        new_pos = (
            jnp.einsum("amc,mc->ac", parent_rot, offset, precision=lax.Precision.HIGHEST)
            + parent_pos
        )
        rot_now = lax.dynamic_update_index_in_dim(rot_now, new_rot, joint, 0)
        pos_now = lax.dynamic_update_index_in_dim(pos_now, new_pos, joint, 0)
        return (rot_now, pos_now)

    glob_rot, glob_pos = lax.fori_loop(1, joint_total, compose, (glob_rot, glob_pos))
    correction = glob_pos - jnp.einsum(
        "jamc,jmc->jac", glob_rot, places, precision=lax.Precision.HIGHEST
    )
    frames = jnp.concatenate(
        [glob_rot.reshape(joint_total, 9, glob_rot.shape[3]), correction], axis=1
    )
    return jnp.transpose(frames, (2, 1, 0))


def dense_weights(joint_index, raw_weights, joint_total):
    shares = raw_weights / jnp.sum(raw_weights, axis=1, keepdims=True)
    matches = joint_index[None, :, :] == jnp.arange(joint_total, dtype=jnp.int32)[:, None, None]
    return jnp.sum(
        jnp.where(matches, shares[None, :, :], jnp.zeros_like(shares)[None, :, :]), axis=2
    )


def apply_frames(blended, shaped_wide):
    coords = []
    for axis_out in range(3):
        value = blended[:, 9 + axis_out]
        for axis_in in range(3):
            value = value + blended[:, 3 * axis_out + axis_in] * shaped_wide[:, axis_in]
        coords.append(value)
    return jnp.stack(coords, axis=1)


def body(
    coeffs,
    shape_basis,
    template,
    regressor,
    quaternions,
    translation,
    parents,
    skin_index,
    skin_raw,
):
    joint_total = regressor.shape[0]
    full_basis = lax.all_gather(shape_basis, "col", axis=0, tiled=True)
    components = full_basis.shape[0]
    vert_count = full_basis.shape[2]
    flat_basis = full_basis.reshape(components, 3 * vert_count)
    base_row = template.reshape(1, 3 * vert_count)
    full_shape = (
        jnp.dot(
            lax.all_gather(coeffs, "vert", axis=0, tiled=True),
            flat_basis,
            preferred_element_type=jnp.float32,
        )
        + base_row
    )
    group_count = full_shape.shape[0]
    shaped_three = full_shape.astype(jnp.bfloat16).reshape(group_count, 3, vert_count)
    partial_value = jnp.einsum(
        "cmv,jv->cmj",
        full_shape.reshape(group_count, 3, vert_count),
        regressor,
        precision=lax.Precision.HIGHEST,
    )
    joints = lax.psum_scatter(partial_value, "vert", scatter_dimension=0, tiled=True)
    own_frames = kinematics(joints, quaternions, translation, parents)
    group_frames = lax.all_gather(own_frames, "vert", axis=0, tiled=True)
    weight_grid = dense_weights(skin_index, skin_raw, joint_total)
    blended = jnp.einsum("cej,jv->cev", group_frames, weight_grid, precision=lax.Precision.HIGHEST)
    posed_local = apply_frames(blended, shaped_three.astype(jnp.float32)).astype(jnp.bfloat16)
    return lax.all_to_all(posed_local, "vert", split_axis=0, concat_axis=2, tiled=True)


def solution(mesh):
    in_specs = (
        P(("vert", "col"), None),
        P("col", None, "vert"),
        P(None, "vert"),
        P(None, "vert"),
        P(("vert", "col"), None, None),
        P(("vert", "col"), None),
        P(),
        P("vert", None),
        P("vert", None),
    )
    out_specs = P(("vert", "col"), None, None)
    return jax.shard_map(body, mesh=mesh, in_specs=in_specs, out_specs=out_specs, check_vma=False)
```

profile of v0, /device:TPU:0, one launch (start us, length us, event | category | flops | bytes accessed | tf_op | source)
XLA Modules:
  0.0 288.7 jit_solution(18105276202222392193)
XLA Ops:
  0.0 0.9 multiply_add_fusion.2
  0.9 0.8 add.183
  1.7 28.1 %all-gather = bf16[8,2,400]{2,1,0:T(2,128)(2,1)S(1)} all-gather(bf16[1,2,400]{2,1,0:T(2,128)(2,1)} %bitcast.166), channel_id=1, replica_groups=mesh['vert'=8,'col'=4] {'vert'}, dimensions={0}, use_global_device_ids=true | all-gather | bytes 14400 | tf_op jit(solution)/shard_map/all_gather | solution.py:105
  29.9 6.5 %all_gather.10 = bf16[400,3,82]{2,1,0:T(4,128)(2,1)S(1)} all-gather(bf16[100,3,82]{2,1,0:T(4,128)(2,1)S(1)} %copy.86), channel_id=1, replica_groups=mesh['vert'=8,'col'=4] {'col'}, dimensions={0}, use_global_device_ids=true | all-gather | bytes 246000 | tf_op jit(solution)/shard_map/all_gather | solution.py:98
  38.1 35.4 %all-reduce.1 = f32[16,3,55]{2,0,1:T(8,128)S(1)} all-reduce(f32[16,3,55]{2,0,1:T(8,128)S(1)} %fusion.8), channel_id=2, replica_groups=mesh['vert'=8,'col'=4] {'vert'}, use_global_device_ids=true, to_apply=%region_0.0.clone | all-reduce | flops 2640 | bytes 21120
  73.6 0.7 copy-done.8
  77.1 169.4 %while.19 = (s32[]{:T(128)}, f32[55,3,3,2]{2,3,1,0:T(2,128)S(1)}, f32[55,3,2]{1,2,0:T(2,128)S(1)}, f32[55,3,3,2]{2,3,1,0:T(2,128)S(1)}, s32[55]{0:T(128)S(1)}, /...) while((s32[]{:T(128)}, f32[55,3,3,2]{2,3,1,0:T(2,128)S(1)}, ...), condition=%wide.region_2.0_spmd, body=%wide.region_1.0_spmd.sunk | while | flops 884 | bytes 9465 | solution.py:58
  80.2 0.7 dynamic_slice.89
  83.3 0.7 dynamic_slice.89
  86.5 0.6 dynamic_slice.89
  89.6 0.7 dynamic_slice.89
  92.7 0.6 dynamic_slice.89
  95.9 0.7 dynamic_slice.89
  99.0 0.6 dynamic_slice.89
  102.2 0.7 dynamic_slice.89
  105.3 0.7 dynamic_slice.89
  108.4 0.6 dynamic_slice.89
  111.6 0.7 dynamic_slice.89
  114.7 0.6 dynamic_slice.89
  117.8 0.7 dynamic_slice.89
  121.0 0.6 dynamic_slice.89
  124.1 0.7 dynamic_slice.89
  127.3 0.7 dynamic_slice.89
  130.4 0.7 dynamic_slice.89
  133.5 0.7 dynamic_slice.89
  136.7 0.6 dynamic_slice.89
  139.8 0.7 dynamic_slice.89
  142.9 0.6 dynamic_slice.89
  146.1 0.7 dynamic_slice.89
  149.2 0.6 dynamic_slice.89
  152.4 0.7 dynamic_slice.89
  155.5 0.7 dynamic_slice.89
  158.6 0.6 dynamic_slice.89
  161.8 0.7 dynamic_slice.89
  164.9 0.6 dynamic_slice.89
  168.0 0.7 dynamic_slice.89
  171.2 0.6 dynamic_slice.89
  174.3 0.7 dynamic_slice.89
  177.5 0.7 dynamic_slice.89
  180.6 0.7 dynamic_slice.89
  183.7 0.7 dynamic_slice.89
  186.9 0.6 dynamic_slice.89
  190.0 0.7 dynamic_slice.89
  193.1 0.6 dynamic_slice.89
  196.3 0.7 dynamic_slice.89
  199.4 0.6 dynamic_slice.89
  202.6 0.7 dynamic_slice.89
  205.7 0.7 dynamic_slice.89
  208.8 0.6 dynamic_slice.89
  212.0 0.7 dynamic_slice.89
  215.1 0.6 dynamic_slice.89
  218.2 0.7 dynamic_slice.89
  221.4 0.6 dynamic_slice.89
  224.5 0.7 dynamic_slice.89
  227.7 0.7 dynamic_slice.89
  230.8 0.7 dynamic_slice.89
  233.9 0.7 dynamic_slice.89
  237.1 0.6 dynamic_slice.89
  240.2 0.7 dynamic_slice.89
  243.3 0.6 dynamic_slice.89
  247.3 30.5 %all_gather.11 = f32[16,12,55]{2,1,0:T(8,128)S(1)} all-gather(f32[2,12,55]{2,1,0:T(8,128)S(1)} %copy.95), channel_id=1, replica_groups=mesh['vert'=8,'col'=4] {'vert'}, dimensions={0}, use_global_device_ids=true | all-gather | bytes 47520 | tf_op jit(solution)/shard_map/all_gather | solution.py:121
  277.9 0.7 copy-done.4
  279.0 8.9 %all_to_all.18 = bf16[8,2,246]{2,1,0:T(2,128)(2,1)S(1)} all-to-all(bf16[8,2,246]{2,1,0:T(2,128)(2,1)S(1)} %reshape.121), channel_id=1, replica_groups=mesh['vert'=8,'col'=4] {'vert'}, dimensions={0} | all-to-all | bytes 15744 | tf_op jit(solution)/shard_map/all_to_all | solution.py:125
  288.0 0.7 all_to_all.16
  (543 shorter events, 38.0 us)
Async XLA Ops:
  0.0 38.0 %copy-start = (f32[55,82]{1,0:T(8,128)S(1)}, f32[55,82]{1,0:T(8,128)}, u32[]{:S(2)}) copy-start(f32[55,82]{1,0:T(8,128)} %param.18) | copy-start | bytes 54124
  0.0 0.9 copy-start.2
  0.0 29.8 %copy-start.1 = (bf16[100,3,82]{0,2,1:T(8,128)(2,1)S(1)}, bf16[100,3,82]{0,2,1:T(8,128)(2,1)}, u32[]{:S(2)}) copy-start(bf16[100,3,82]{0,2,1:T(8,128)(2,1)} %param.16) | copy-start | bytes 147604
  37.0 0.7 copy-start.6
  73.6 0.7 copy-start.8
  75.7 0.7 copy-start.5
  76.4 0.7 copy-start.7
  247.3 30.6 %copy-start.3 = (f32[82,4]{0,1:T(4,128)S(1)}, f32[82,4]{0,1:T(4,128)}, u32[]{:S(2)}) copy-start(f32[82,4]{0,1:T(4,128)} %param.23) | copy-start | bytes 3940
  277.9 0.7 copy-start.4
where the time goes:
time: 291 us; the launch traced here: 289 us
  blocking collectives  109 us (37%)
  loops' own time  102 us (35%)
  local copies, waits for them, and re-layouts  54.8 us (19%)
  matrix products  19.3 us (7%)
    another operation x1, loops' own time, kinematics(): lax.fori_loop(1, joint_total, compose, (glob_rot, glob_pos))  102 us
    unnamed x1, blocking collectives  35.4 us
    dynamic_slice x54, local copies, waits for them, and re-layouts, compose(): parent = lax.dynamic_index_in_dim(parents, joint, 0, keepdims=False)  35.1 us
    all_gather x1, blocking collectives, body(): group_frames = lax.all_gather(own_frames, 'vert', axis=0, tiled=True)  30.5 us
    all_gather x1, blocking collectives, body(): lax.all_gather(coeffs, 'vert', axis=0, tiled=True)  28.1 us
    dot_general x54, matrix products, compose(): jnp.einsum('amc,mbc->abc', parent_rot, local_rot, precision=lax.Precision...  11.1 us
    all_to_all x1, blocking collectives, body(): lax.all_to_all(posed_local, 'vert', split_axis=0, concat_axis=2, tiled=True)  8.89 us
    dot_general x54, matrix products, compose(): jnp.einsum('amc,mc->ac', parent_rot, offset, precision=lax.Precision.HIGH...  7.68 us

commit v1 on v0

v1 whole, which is shorter than its diff:
```python
import functools

import jax
import jax.numpy as jnp
from jax import lax
from jax.experimental import pallas as pl
from jax.experimental.pallas import tpu as pltpu
from jax.sharding import PartitionSpec as P

MESH = pl.DeviceIdType.MESH
LANES = 128
HALF = 64
SUB = 8
F32 = jnp.float32
BF16 = jnp.bfloat16
EXACT = lax.Precision.HIGHEST


def iota(shape, dim):
    return lax.broadcasted_iota(jnp.int32, shape, dim)


def dot(a, b, precision=None):
    return jnp.dot(a, b, precision=precision, preferred_element_type=F32)


def dot_nt(a, b, precision=None):
    return lax.dot_general(a, b, (((1,), (1,)), ((), ())), precision=precision, preferred_element_type=F32)


def each(count, step):
    if count <= 16:
        for k in range(1, count):
            step(k)
    else:

        def one(k, carry):
            step(k)
            return carry

        lax.fori_loop(1, count, one, 0)


def kernel(
    n_vert,
    n_col,
    parents_ref,
    coeffs_ref,
    basis_ref,
    template_ref,
    regressor_ref,
    quat_ref,
    shift_ref,
    index_ref,
    raw_ref,
    out_ref,
    msg,
    bas,
    part,
    sums_in,
    sent,
    got,
    reg_lo,
    reg_hi,
    state,
    diff,
    locals_ref,
    tree,
    msg_s,
    msg_r,
    bas_s,
    bas_r,
    part_s,
    part_r,
    pos_s,
    pos_r,
):
    me = lax.axis_index("vert")
    col = lax.axis_index("col")
    own = coeffs_ref.shape[0]
    comps = basis_ref.shape[2]
    block = basis_ref.shape[1]
    joints = regressor_ref.shape[0]
    group = min(n_vert, LANES // SUB)
    n_group = n_vert // group
    rows = group * SUB
    chars = group * own
    fold = chars // 2
    msg_rows = chars + fold

    barrier = pltpu.get_barrier_semaphore()

    def vert_peer(k):
        return (lax.rem(me + k, n_vert), col)

    def col_peer(k):
        return (me, lax.rem(col + k, n_col))

    each(n_vert, lambda k: pl.semaphore_signal(barrier, inc=1, device_id=vert_peer(k), device_id_type=MESH))
    each(n_col, lambda k: pl.semaphore_signal(barrier, inc=1, device_id=col_peer(k), device_id_type=MESH))

    msg[me] = jnp.zeros(msg.shape[1:], F32)
    for c in range(own):
        msg[me, 4 * c : 4 * c + 4, 0:joints] = quat_ref[c]
    coeff_rows = coeffs_ref[...].astype(F32)
    for kb in range(n_col):
        msg[me, SUB + own * kb : SUB + own * (kb + 1), 0:comps] = coeff_rows[:, kb * comps : (kb + 1) * comps]
    msg[me, 2 * SUB : 2 * SUB + own, 0:3] = shift_ref[...]
    bas[col] = basis_ref[...]

    reg_lo[...] = jnp.zeros(reg_lo.shape, F32)
    reg_hi[...] = jnp.zeros(reg_hi.shape, F32)
    reg_lo[0:joints, :] = regressor_ref[...]
    reg_hi[HALF : HALF + joints, :] = regressor_ref[...]
    sent[...] = jnp.zeros(sent.shape, F32)
    tree[...] = jnp.zeros(tree.shape, F32)
    state[...] = jnp.zeros(state.shape, F32)
    diff[...] = jnp.zeros(diff.shape, F32)
    lane8 = iota((SUB, LANES), 1)
    sub8 = iota((SUB, LANES), 0)
    axis_lane = jnp.minimum((lane8 % SUB) // own, 2)
    raw = raw_ref[...]
    shares = raw / jnp.sum(raw, axis=0, keepdims=True)
    joint_row = iota((HALF, block), 0)
    weights = jnp.zeros((HALF, block), F32)
    for i in range(index_ref.shape[0]):
        weights = weights + jnp.where(index_ref[i : i + 1, :] == joint_row, shares[i : i + 1, :], 0.0)

    pl.semaphore_wait(barrier, n_vert + n_col - 2)

    def copies(src, dst, send, recv, peer_of):
        def make(k):
            return pltpu.make_async_remote_copy(
                src_ref=src, dst_ref=dst, send_sem=send.at[k], recv_sem=recv.at[k], device_id=peer_of(k), device_id_type=MESH
            )

        return make

    msg_copy = copies(msg.at[me], msg.at[me], msg_s, msg_r, vert_peer)
    bas_copy = copies(basis_ref, bas.at[col], bas_s, bas_r, col_peer)
    each(n_vert, lambda k: msg_copy(k).start())
    each(n_col, lambda k: bas_copy(k).start())
    each(n_vert, lambda k: msg_copy(k).wait_recv())

    e_row = iota((chars + rows, rows), 0)
    e_col = iota((chars + rows, rows), 1)
    r_row = jnp.where(e_row < chars, 0, e_row - chars)
    source = jnp.where(e_row < chars, e_row // own, r_row // SUB)
    member = jnp.where(e_row < chars, e_row % own, r_row % own)
    coeff_blocks = []
    for g in range(n_group):
        table = msg[g * group : (g + 1) * group, SUB : 2 * SUB, :].reshape(rows, LANES).astype(BF16)
        picks = [(e_col == source * SUB + kb * own + member) for kb in range(n_col)]
        coeff_blocks.append([dot(p.astype(F32).astype(BF16), table).astype(BF16)[:, 0:comps] for p in picks])

    q_row = iota((LANES, rows), 0)
    q_col = iota((LANES, rows), 1)
    q_base = ((q_row // SUB) % group) * SUB + (q_row % own) * 4
    for g in range(n_group):
        quats = msg[g * group : (g + 1) * group, 0:SUB, :].reshape(rows, LANES)
        w, x, y, z = [
            jnp.transpose(dot((q_col == q_base + comp).astype(F32), quats, EXACT))[0:HALF] for comp in range(4)
        ]
        s = 2.0 / (w * w + x * x + y * y + z * z)
        matrix = [
            [1.0 - s * (y * y + z * z), s * (x * y - w * z), s * (x * z + w * y)],
            [s * (x * y + w * z), 1.0 - s * (x * x + z * z), s * (y * z - w * x)],
            [s * (x * z - w * y), s * (y * z + w * x), 1.0 - s * (x * x + y * y)],
        ]
        for m in range(3):
            for b in range(3):
                locals_ref[g, m, pl.ds(b, HALF, stride=SUB), :] = matrix[m][b]

    each(n_col, lambda k: bas_copy(k).wait_recv())
    shaped = []
    for g in range(n_group):
        full = []
        for m in range(3):
            total = template_ref[m : m + 1, :]
            for kb in range(n_col):
                total = total + dot_nt(coeff_blocks[g][kb], bas[kb, m])
            full.append(total)
        low = jnp.concatenate([full[0][0:chars], full[2][0:fold]], axis=0)
        high = jnp.concatenate([full[1][0:chars], full[2][fold:chars]], axis=0)
        part[g] = dot_nt(low, reg_lo[...], EXACT) + dot_nt(high, reg_hi[...], EXACT)
        shaped.append([f[chars:].astype(BF16).astype(F32) for f in full])

    part_copy = copies(part, sums_in.at[me], part_s, part_r, vert_peer)
    each(n_vert, lambda k: part_copy(k).start())
    sums_in[me] = part[...]

    def compose(j, g, above):
        at = pl.multiple_of(j * SUB, SUB)
        new = jnp.zeros((SUB, LANES), F32)
        for m in range(3):
            new = new + jnp.broadcast_to(above[m : m + 1, :], (SUB, LANES)) * locals_ref[g, m, pl.ds(at, SUB), :]
        mine = above + (lane8 % HALF == j).astype(F32)
        new = jnp.where(sub8 < 3, new, jnp.where(sub8 == 3, mine, 0.0))
        if isinstance(j, int):
            new = new + jnp.where((sub8 == 3) & (lane8 == joints), 1.0, 0.0)
        tree[g, j] = new
        state[g, pl.ds(at, SUB), :] = new
        diff[g, pl.ds(at, SUB), :] = above - new

    def descend(j, carry):
        for g in range(n_group):
            compose(j, g, tree[g, parents_ref[j]])
        return carry

    for g in range(n_group):
        compose(0, g, (axis_lane == sub8).astype(F32))
    lax.fori_loop(1, joints, descend, 0)

    def plane(ref, g, m):
        return ref[g, pl.ds(m, HALF, stride=SUB), :]

    weights_up = dot(jnp.transpose(plane(state, 0, 3)), weights, EXACT)
    lane = iota((rows, LANES), 1)
    row = iota((rows, LANES), 0)
    row_char = (row // SUB) * own + row % own
    row_axis = jnp.minimum((row % SUB) // own, 2)
    t_row = iota((rows, rows), 0)
    t_col = iota((rows, rows), 1)
    t_pick = (t_col == (t_row // SUB) * SUB + t_row % own).astype(F32)
    gains, turned, moved = [], [], []
    for g in range(n_group):
        gain = jnp.transpose(jnp.concatenate([plane(diff, g, 0), plane(diff, g, 1)], axis=0))[0:rows]
        last = jnp.concatenate([plane(diff, g, 2)] * 2, axis=0)
        last = jnp.transpose(last)[0:rows]
        last = jnp.where((lane < HALF) == (row_char < fold), last, 0.0)
        gains.append((gain, last))
        shift = dot(t_pick, msg[g * group : (g + 1) * group, 2 * SUB : 3 * SUB, :].reshape(rows, LANES), EXACT)
        shift = jnp.sum(jnp.where(lane == row_axis, shift, 0.0), axis=1, keepdims=True)
        moved.append(jnp.where(lane == joints, shift, 0.0))
        turn = jnp.zeros((rows, block), F32)
        for m in range(3):
            if m == 0:
                pair = jnp.transpose(jnp.concatenate([plane(state, g, 0), plane(state, g, 1)], axis=0))[0:rows]
                spun = pair[:, 0:HALF]
            elif m == 1:
                spun = pair[:, HALF:LANES]
            else:
                spun = jnp.transpose(jnp.concatenate([plane(state, g, 2)] * 2, axis=0))[0:rows, 0:HALF]
            turn = turn + dot(spun, weights, EXACT) * shaped[g][m]
        turned.append(turn)

    x_row = iota((2 * rows, msg_rows), 0)
    x_col = iota((2 * rows, msg_rows), 1)
    x_r = x_row % rows
    x_char = (x_r // SUB) * own + x_r % own
    spread = (x_col == jnp.where(x_row < rows, x_char, chars + x_char % fold)).astype(F32)
    each(n_vert, lambda k: part_copy(k).wait_recv())
    for g in range(n_group):
        if n_vert <= 16:
            summed = sums_in[0, g]
            for i in range(1, n_vert):
                summed = summed + sums_in[i, g]
        else:
            summed = lax.fori_loop(1, n_vert, lambda i, a: a + sums_in[i, g], sums_in[0, g])
        wide = dot(spread, summed, EXACT)
        term = gains[g][0] * wide[0:rows] + gains[g][1] * wide[rows:] + moved[g]
        posed = turned[g] + dot(term, weights_up, EXACT)
        sent[g * group : (g + 1) * group, :, 0:block] = posed.reshape(group, SUB, block)

    def pos_copy(k):
        target = lax.rem(me + k, n_vert)
        return pltpu.make_async_remote_copy(
            src_ref=sent.at[target],
            dst_ref=got.at[me],
            send_sem=pos_s.at[k],
            recv_sem=pos_r.at[k],
            device_id=(target, col),
            device_id_type=MESH,
        )

    each(n_vert, lambda k: pos_copy(k).start())
    got[me] = sent[me]
    each(n_vert, lambda k: pos_copy(k).wait_recv())

    n_cols = -(-n_vert * block // LANES) + 1
    columns = [None] * n_cols

    def put(q, value):
        columns[q] = value if columns[q] is None else columns[q] + value

    for i in range(n_vert):
        q, r = divmod(i * block, LANES)
        tile = got[i]
        if r:
            tile = pltpu.roll(tile, r, 1)
        if r + block > LANES:
            put(q, jnp.where(lane8 >= r, tile, 0.0))
            put(q + 1, jnp.where(lane8 < r, tile, 0.0))
        else:
            put(q, tile)
    width = n_vert * block
    for q in range(n_cols):
        size = min(LANES, width - q * LANES)
        if size > 0:
            value = columns[q].astype(BF16)
            for a in range(3):
                out_ref[a, :, q * LANES : q * LANES + size] = value[own * a : own * (a + 1), 0:size]

    each(n_vert, lambda k: msg_copy(k).wait_send())
    each(n_col, lambda k: bas_copy(k).wait_send())
    each(n_vert, lambda k: part_copy(k).wait_send())
    each(n_vert, lambda k: pos_copy(k).wait_send())


def body(n_vert, n_col, coeffs, shape_basis, template, regressor, quaternions, translation, parents, skin_index, skin_raw):
    own = coeffs.shape[0]
    comps, _, block = shape_basis.shape
    joints = regressor.shape[0]
    group = min(n_vert, LANES // SUB)
    n_group = n_vert // group
    msg_rows = group * own + group * own // 2
    vmem = pl.BlockSpec(memory_space=pltpu.VMEM)
    dma = pltpu.SemaphoreType.DMA
    out = pl.pallas_call(
        functools.partial(kernel, n_vert, n_col),
        out_shape=jax.ShapeDtypeStruct((3, own, n_vert * block), BF16),
        in_specs=[pl.BlockSpec(memory_space=pltpu.SMEM)] + [vmem] * 8,
        out_specs=vmem,
        scratch_shapes=[
            pltpu.VMEM((n_vert, 3 * SUB, LANES), F32),
            pltpu.VMEM((n_col, 3, block, comps), BF16),
            pltpu.VMEM((n_group, msg_rows, LANES), F32),
            pltpu.VMEM((n_vert, n_group, msg_rows, LANES), F32),
            pltpu.VMEM((n_vert, SUB, LANES), F32),
            pltpu.VMEM((n_vert, SUB, LANES), F32),
            pltpu.VMEM((LANES, block), F32),
            pltpu.VMEM((LANES, block), F32),
            pltpu.VMEM((n_group, HALF * SUB, LANES), F32),
            pltpu.VMEM((n_group, HALF * SUB, LANES), F32),
            pltpu.VMEM((n_group, 3, HALF * SUB, LANES), F32),
            pltpu.VMEM((n_group, joints, SUB, LANES), F32),
            dma((n_vert,)),
            dma((n_vert,)),
            dma((n_col,)),
            dma((n_col,)),
            dma((n_vert,)),
            dma((n_vert,)),
            dma((n_vert,)),
            dma((n_vert,)),
        ],
        compiler_params=pltpu.CompilerParams(collective_id=0, has_side_effects=True),
    )(
        parents,
        coeffs,
        jnp.transpose(shape_basis, (1, 2, 0)),
        template,
        regressor,
        quaternions,
        translation,
        jnp.transpose(skin_index),
        jnp.transpose(skin_raw),
    )
    return jnp.transpose(out, (1, 0, 2))


def solution(mesh):
    in_specs = (
        P(("vert", "col"), None),
        P("col", None, "vert"),
        P(None, "vert"),
        P(None, "vert"),
        P(("vert", "col"), None, None),
        P(("vert", "col"), None),
        P(),
        P("vert", None),
        P("vert", None),
    )
    out_specs = P(("vert", "col"), None, None)
    step = functools.partial(body, mesh.shape["vert"], mesh.shape["col"])
    return jax.shard_map(step, mesh=mesh, in_specs=in_specs, out_specs=out_specs, check_vma=False)
```

time: 291 us -> 24.3 us (0.08)
  blocking collectives: 109 us -> 0 us
  loops' own time: 102 us -> 0 us
  local copies, waits for them, and re-layouts: 54.8 us -> 1.31 us
  Pallas kernels: 0 us -> 22.8 us
  matrix products: 19.3 us -> 0 us
    another operation x1 -> x0, loops' own time: 102 us -> none  [kinematics(): lax.fori_loop(1, joint_total, compose, (glob_rot, glob_pos))]
    all_gather x3 -> x0, blocking collectives: 65.1 us -> none  [the longest x1 30.5 us: body(): group_frames = lax.all_gather(own_frames, 'vert', axis=0, tiled=True)]
    unnamed x1 -> x0, blocking collectives: 35.4 us -> none
    dynamic_slice x54 -> x0, local copies, waits for them, and re-layouts: 35.1 us -> none  [compose(): parent = lax.dynamic_index_in_dim(parents, joint, 0, keepdims=False)]
    pallas_call x0 -> x1, Pallas kernels: none -> 22.8 us  [body(): pl.pallas_call(functools.partial(kernel, n_vert, n_col), out_shape=jax.Sh...]
    dot_general x111 -> x0, matrix products: 19.3 us -> none  [the longest x54 11.1 us: compose(): jnp.einsum('amc,mbc->abc', parent_rot, local_rot, precision=lax.Precision...]
    all_to_all x1 -> x0, blocking collectives: 8.89 us -> none  [body(): lax.all_to_all(posed_local, 'vert', split_axis=0, concat_axis=2, tiled=True)]
    squeeze x108 -> x0, local copies, waits for them, and re-layouts: 5.97 us -> none  [compose(): parent_rot = lax.dynamic_index_in_dim(rot_now, parent, 0, keepdims=False)]
where the time goes in v1:
time: 24.3 us; the launch traced here: 24.1 us
  Pallas kernels  22.8 us (94%)
  local copies, waits for them, and re-layouts  1.31 us (5%)
    pallas_call x1, Pallas kernels, body(): pl.pallas_call(functools.partial(kernel, n_vert, n_col), out_shape=jax.Sh...  22.8 us
    unnamed x1, local copies, waits for them, and re-layouts  1.31 us

profile of v1, /device:TPU:0, one launch (start us, length us, event | category | flops | bytes accessed | tf_op | source)
XLA Modules:
  0.0 24.1 jit_solution(11841234715388635048)
XLA Ops:
  0.0 22.8 %shard_map.91 = bf16[3,2,656]{2,1,0:T(2,128)(2,1)} custom-call(s32[55]{0:T(128)} %parents_ref.1, bf16[2,400]{1,0:T(2,128)(2,1)} %coeffs_ref.1, bf16[3,82,100]{2,1,0:T(8,128)(2,1)} %bitcast.4, f32[3,82]{1,0:T(4,128)} %template_ref.1, f32[55,82]{1,0:T(8,128)} %regressor_ref.1, f32[2,4,55]{2,1,0:T(4,128)} %quat_ref.1, f32[2,3]{1,0:T(2,128)} %shift_ref.1, ...), custom_call_target="tpu_custom_call" | custom-call | tf_op jit(solution)/shard_map/pallas_call | solution.py:319
  22.8 1.3 %copy.11 = bf16[2,3,656]{2,0,1:T(2,128)(2,1)} copy(bf16[2,3,656]{2,0,1:T(2,128)(2,1)} %bitcast.5) | data formatting | bytes 15744

commit v2 on v1

v2 whole, which is shorter than its diff:
```python
import functools

import jax
import jax.numpy as jnp
from jax import lax
from jax.experimental import pallas as pl
from jax.experimental.pallas import tpu as pltpu
from jax.sharding import PartitionSpec as P

MESH = pl.DeviceIdType.MESH
LANES = 128
HALF = 64
SUB = 8
F32 = jnp.float32
BF16 = jnp.bfloat16
EXACT = lax.Precision.HIGHEST


def iota(shape, dim):
    return lax.broadcasted_iota(jnp.int32, shape, dim)


def dot(a, b, precision=None):
    return jnp.dot(a, b, precision=precision, preferred_element_type=F32)


def dot_nt(a, b, precision=None):
    return lax.dot_general(a, b, (((1,), (1,)), ((), ())), precision=precision, preferred_element_type=F32)


def each(count, step):
    if count <= 16:
        for k in range(1, count):
            step(k)
    else:

        def one(k, carry):
            step(k)
            return carry

        lax.fori_loop(1, count, one, 0)


def kernel(
    n_vert,
    n_col,
    parents_hbm,
    coeffs_hbm,
    basis_hbm,
    template_hbm,
    regressor_hbm,
    quat_hbm,
    shift_hbm,
    index_hbm,
    raw_hbm,
    out_ref,
    parents,
    coeff_in,
    bas,
    template,
    regressor,
    quat,
    shift,
    index_in,
    raw_in,
    quat_rows,
    coeff_rows,
    sent,
    got,
    tree,
    state,
    diff,
    locals_ref,
    weights,
    local_s,
    coeff_s,
    coeff_r,
    bas_s,
    bas_r,
    index_s,
    index_r,
    raw_s,
    raw_r,
    sent_s,
    sent_r,
):
    me = lax.axis_index("vert")
    col = lax.axis_index("col")
    own, _ = coeffs_hbm.shape
    _, block, comps = basis_hbm.shape
    joints = regressor_hbm.shape[0]
    rows = n_vert * SUB

    barrier = pltpu.get_barrier_semaphore()

    def vert_peer(k):
        return (lax.rem(me + k, n_vert), col)

    def col_peer(k):
        return (me, lax.rem(col + k, n_col))

    each(n_vert, lambda k: pl.semaphore_signal(barrier, inc=1, device_id=vert_peer(k), device_id_type=MESH))
    each(n_col, lambda k: pl.semaphore_signal(barrier, inc=1, device_id=col_peer(k), device_id_type=MESH))

    pairs = [
        (coeffs_hbm, coeff_in.at[me]),
        (basis_hbm, bas.at[col]),
        (index_hbm, index_in.at[me]),
        (raw_hbm, raw_in.at[me]),
        (parents_hbm, parents),
        (quat_hbm, quat),
        (shift_hbm, shift),
        (template_hbm, template),
        (regressor_hbm, regressor),
    ]
    loads = [pltpu.make_async_copy(src, dst, local_s.at[i]) for i, (src, dst) in enumerate(pairs)]
    for load in loads:
        load.start()

    sub8 = iota((SUB, LANES), 0)
    lane8 = iota((SUB, LANES), 1)
    axis_lane = jnp.minimum((lane8 % SUB) // own, 2)
    quat_rows[...] = jnp.zeros(quat_rows.shape, F32)
    weights[...] = jnp.zeros(weights.shape, F32)
    tree[...] = jnp.zeros(tree.shape, F32)
    state[...] = jnp.zeros(state.shape, F32)
    diff[...] = jnp.zeros(diff.shape, F32)
    sent[...] = jnp.zeros(sent.shape, F32)
    for load in loads:
        load.wait()

    def copies(src, dst, send, recv, peer_of):
        def make(k):
            return pltpu.make_async_remote_copy(
                src_ref=src, dst_ref=dst, send_sem=send.at[k], recv_sem=recv.at[k], device_id=peer_of(k), device_id_type=MESH
            )

        return make

    coeff_copy = copies(coeff_in.at[me], coeff_in.at[me], coeff_s, coeff_r, vert_peer)
    bas_copy = copies(bas.at[col], bas.at[col], bas_s, bas_r, col_peer)
    index_copy = copies(index_in.at[me], index_in.at[me], index_s, index_r, vert_peer)
    raw_copy = copies(raw_in.at[me], raw_in.at[me], raw_s, raw_r, vert_peer)

    pl.semaphore_wait(barrier, n_vert + n_col - 2)
    each(n_vert, lambda k: coeff_copy(k).start())
    each(n_col, lambda k: bas_copy(k).start())
    each(n_vert, lambda k: index_copy(k).start())
    each(n_vert, lambda k: raw_copy(k).start())

    for c in range(own):
        quat_rows[4 * c : 4 * c + 4, 0:joints] = quat[c]
    q_row = iota((LANES, SUB), 0)
    q_col = iota((LANES, SUB), 1)
    w, x, y, z = [
        jnp.transpose(dot((q_col == (q_row % own) * 4 + comp).astype(F32), quat_rows[...], EXACT))[0:HALF] for comp in range(4)
    ]
    s = 2.0 / (w * w + x * x + y * y + z * z)
    matrix = [
        [1.0 - s * (y * y + z * z), s * (x * y - w * z), s * (x * z + w * y)],
        [s * (x * y + w * z), 1.0 - s * (x * x + z * z), s * (y * z - w * x)],
        [s * (x * z - w * y), s * (y * z + w * x), 1.0 - s * (x * x + y * y)],
    ]
    for m in range(3):
        for b in range(3):
            locals_ref[m, pl.ds(b, HALF, stride=SUB), :] = matrix[m][b]

    def compose(j, above):
        at = pl.multiple_of(j * SUB, SUB)
        new = jnp.zeros((SUB, LANES), F32)
        for m in range(3):
            new = new + jnp.broadcast_to(above[m : m + 1, :], (SUB, LANES)) * locals_ref[m, pl.ds(at, SUB), :]
        mine = above + (lane8 % HALF == j).astype(F32)
        new = jnp.where(sub8 < 3, new, jnp.where(sub8 == 3, mine, 0.0))
        if isinstance(j, int):
            new = new + jnp.where((sub8 == 3) & (lane8 == joints), 1.0, 0.0)
        tree[j] = new
        state[pl.ds(at, SUB), :] = new
        diff[pl.ds(at, SUB), :] = above - new

    def descend(j, carry):
        compose(j, tree[parents[j]])
        return carry

    compose(0, (axis_lane == sub8).astype(F32))
    lax.fori_loop(1, joints, descend, 0)

    def flipped(ref, m, n):
        value = ref[pl.ds(m, HALF, stride=SUB), :]
        return jnp.transpose(jnp.concatenate([value, value], axis=0))[0:n]

    gains = [flipped(diff, m, SUB) for m in range(3)]
    gains = [jnp.where(lane8 < HALF, gain, 0.0) for gain in gains]
    factors = jnp.concatenate(
        [flipped(state, m, SUB)[:, 0:HALF] for m in range(3)] + [flipped(state, 3, HALF)[:, 0:HALF]], axis=0
    )
    moves = jnp.concatenate([shift[...]] * (SUB // own), axis=0)
    m_axis = jnp.minimum(iota(moves.shape, 0) // own, 2)
    moves = jnp.sum(jnp.where(iota(moves.shape, 1) == m_axis, moves, 0.0), axis=1, keepdims=True)
    moves = jnp.where(lane8 == joints, moves, 0.0)

    each(n_vert, lambda k: coeff_copy(k).wait_recv())
    for i in range(n_vert):
        one = coeff_in[i].astype(F32)
        coeff_rows[i * SUB : (i + 1) * SUB, 0 : n_col * comps] = jnp.concatenate([one] * (SUB // own), axis=0)
    blocks = [coeff_rows[:, kb * comps : (kb + 1) * comps].astype(BF16) for kb in range(n_col)]

    each(n_col, lambda k: bas_copy(k).wait_recv())
    r_axis = jnp.minimum((iota((rows, block), 0) % SUB) // own, 2)
    full = jnp.zeros((rows, block), F32)
    for m in range(3):
        total = template[m : m + 1, :]
        for kb in range(n_col):
            total = total + dot_nt(blocks[kb], bas[kb, m])
        full = jnp.where(r_axis == m, total, full)
    share = dot_nt(full, regressor[...], EXACT)
    sent[:, 0, :, 0:block] = full.astype(BF16).astype(F32).reshape(n_vert, SUB, block)
    sent[:, 1, :, 0:joints] = share.reshape(n_vert, SUB, joints)

    def sent_copy(k):
        target = lax.rem(me + k, n_vert)
        return pltpu.make_async_remote_copy(
            src_ref=sent.at[target],
            dst_ref=got.at[me],
            send_sem=sent_s.at[k],
            recv_sem=sent_r.at[k],
            device_id=(target, col),
            device_id_type=MESH,
        )

    each(n_vert, lambda k: sent_copy(k).start())
    got[me] = sent[me]

    each(n_vert, lambda k: index_copy(k).wait_recv())
    each(n_vert, lambda k: raw_copy(k).wait_recv())
    joint_row = iota((HALF, block), 0)
    for i in range(n_vert):
        raw = raw_in[i]
        raw = raw / jnp.sum(raw, axis=0, keepdims=True)
        index = index_in[i]
        grid = jnp.zeros((HALF, block), F32)
        for slot in range(raw.shape[0]):
            grid = jnp.where(index[slot : slot + 1, :] == joint_row, raw[slot : slot + 1, :], grid)
        weights[:, i * LANES : i * LANES + block] = grid
    blended = dot(factors, weights[...], EXACT)
    turns = [blended[m * SUB : (m + 1) * SUB] for m in range(3)]
    upper = blended[3 * SUB :]
    upper_hi = upper.astype(BF16)
    upper_lo = (upper - upper_hi.astype(F32)).astype(BF16)
    upper_all = jnp.concatenate([upper_hi, upper_lo, upper_hi], axis=0)

    def rows_of(tile):
        spun = [tile] + [pltpu.roll(tile, own * q, 0) for q in range(1, SUB // own)]
        count = SUB // own
        result = []
        for m in range(3):
            value = spun[(-m) % count]
            for q in range(1, count):
                value = jnp.where(sub8 // own == q, spun[(q - m) % count], value)
            result.append(value)
        return result

    each(n_vert, lambda k: sent_copy(k).wait_recv())
    summed = got[0, 1]
    for i in range(1, n_vert):
        summed = summed + got[i, 1]
    places = rows_of(summed)
    term = moves
    for m in range(3):
        term = term + gains[m] * places[m]
    term_hi = term.astype(BF16)
    term_lo = (term - term_hi.astype(F32)).astype(BF16)
    term_all = jnp.concatenate([term_hi[:, 0:HALF], term_hi[:, 0:HALF], term_lo[:, 0:HALF]], axis=1)
    moved = dot(term_all, upper_all)

    n_cols = -(-n_vert * block // LANES) + 1
    columns = [None] * n_cols

    def put(q, value):
        columns[q] = value if columns[q] is None else columns[q] + value

    for i in range(n_vert):
        q, r = divmod(i * block, LANES)
        at = slice(i * LANES, (i + 1) * LANES)
        shaped = rows_of(got[i, 0])
        tile = moved[:, at]
        for m in range(3):
            tile = tile + turns[m][:, at] * shaped[m]
        if r:
            tile = pltpu.roll(tile, r, 1)
        if r + block > LANES:
            put(q, jnp.where(lane8 >= r, tile, 0.0))
            put(q + 1, jnp.where(lane8 < r, tile, 0.0))
        else:
            put(q, tile)
    width = n_vert * block
    for q in range(n_cols):
        size = min(LANES, width - q * LANES)
        if size > 0:
            value = columns[q].astype(out_ref.dtype)
            for a in range(3):
                out_ref[a, :, q * LANES : q * LANES + size] = value[own * a : own * (a + 1), 0:size]

    each(n_vert, lambda k: coeff_copy(k).wait_send())
    each(n_col, lambda k: bas_copy(k).wait_send())
    each(n_vert, lambda k: index_copy(k).wait_send())
    each(n_vert, lambda k: raw_copy(k).wait_send())
    each(n_vert, lambda k: sent_copy(k).wait_send())


def body(n_vert, n_col, coeffs, shape_basis, template, regressor, quaternions, translation, parents, skin_index, skin_raw):
    own, total = coeffs.shape
    comps, _, block = shape_basis.shape
    joints = regressor.shape[0]
    slots = skin_index.shape[1]
    vmem = pl.BlockSpec(memory_space=pltpu.VMEM)
    anywhere = pl.BlockSpec(memory_space=pl.ANY)
    dma = pltpu.SemaphoreType.DMA
    out = pl.pallas_call(
        functools.partial(kernel, n_vert, n_col),
        out_shape=jax.ShapeDtypeStruct((3, own, n_vert * block), BF16),
        in_specs=[anywhere] * 9,
        out_specs=vmem,
        scratch_shapes=[
            pltpu.SMEM((joints,), jnp.int32),
            pltpu.VMEM((n_vert, own, total), BF16),
            pltpu.VMEM((n_col, 3, block, comps), BF16),
            pltpu.VMEM((3, block), F32),
            pltpu.VMEM((joints, block), F32),
            pltpu.VMEM((own, 4, joints), F32),
            pltpu.VMEM((own, 3), F32),
            pltpu.VMEM((n_vert, slots, block), jnp.int32),
            pltpu.VMEM((n_vert, slots, block), F32),
            pltpu.VMEM((SUB, LANES), F32),
            pltpu.VMEM((n_vert * SUB, total), F32),
            pltpu.VMEM((n_vert, 2, SUB, LANES), F32),
            pltpu.VMEM((n_vert, 2, SUB, LANES), F32),
            pltpu.VMEM((joints, SUB, LANES), F32),
            pltpu.VMEM((HALF * SUB, LANES), F32),
            pltpu.VMEM((HALF * SUB, LANES), F32),
            pltpu.VMEM((3, HALF * SUB, LANES), F32),
            pltpu.VMEM((HALF, n_vert * LANES), F32),
            dma((9,)),
            dma((n_vert,)),
            dma((n_vert,)),
            dma((n_col,)),
            dma((n_col,)),
            dma((n_vert,)),
            dma((n_vert,)),
            dma((n_vert,)),
            dma((n_vert,)),
            dma((n_vert,)),
            dma((n_vert,)),
        ],
        compiler_params=pltpu.CompilerParams(collective_id=0, has_side_effects=True),
    )(
        parents,
        coeffs,
        jnp.transpose(shape_basis, (1, 2, 0)),
        template,
        regressor,
        quaternions,
        translation,
        jnp.transpose(skin_index),
        jnp.transpose(skin_raw),
    )
    return jnp.transpose(out, (1, 0, 2))


def solution(mesh):
    in_specs = (
        P(("vert", "col"), None),
        P("col", None, "vert"),
        P(None, "vert"),
        P(None, "vert"),
        P(("vert", "col"), None, None),
        P(("vert", "col"), None),
        P(),
        P("vert", None),
        P("vert", None),
    )
    out_specs = P(("vert", "col"), None, None)
    step = functools.partial(body, mesh.shape["vert"], mesh.shape["col"])
    return jax.shard_map(step, mesh=mesh, in_specs=in_specs, out_specs=out_specs, check_vma=False)
```

time: 24.3 us -> 17.9 us (0.74)
  Pallas kernels: 22.8 us -> 16.3 us
    pallas_call x1, Pallas kernels: 22.8 us -> 16.3 us  [body(): pl.pallas_call(functools.partial(kernel, n_vert, n_col), out_shape=jax.Sh...]
where the time goes in v2:
time: 17.9 us; the launch traced here: 17.6 us
  Pallas kernels  16.3 us (91%)
  local copies, waits for them, and re-layouts  1.31 us (7%)
    pallas_call x1, Pallas kernels, body(): pl.pallas_call(functools.partial(kernel, n_vert, n_col), out_shape=jax.Sh...  16.3 us
    unnamed x1, local copies, waits for them, and re-layouts  1.31 us

profile of v2, /device:TPU:0, one launch (start us, length us, event | category | flops | bytes accessed | tf_op | source)
XLA Modules:
  0.0 17.6 jit_solution(7328930086125959406)
XLA Ops:
  0.0 16.3 %shard_map.91 = bf16[3,2,656]{2,1,0:T(2,128)(2,1)} custom-call(s32[55]{0:T(128)} %parents_hbm.1, bf16[2,400]{1,0:T(2,128)(2,1)} %coeffs_hbm.1, bf16[3,82,100]{2,1,0:T(8,128)(2,1)} %bitcast.4, f32[3,82]{1,0:T(4,128)} %template_hbm.1, f32[55,82]{1,0:T(8,128)} %regressor_hbm.1, f32[2,4,55]{2,1,0:T(4,128)} %quat_hbm.1, f32[2,3]{1,0:T(2,128)} %shift_hbm.1, ...), custom_call_target="tpu_custom_call" | custom-call | tf_op jit(solution)/shard_map/pallas_call | solution.py:319
  16.3 1.3 %copy.11 = bf16[2,3,656]{2,0,1:T(2,128)(2,1)} copy(bf16[2,3,656]{2,0,1:T(2,128)(2,1)} %bitcast.5) | data formatting | bytes 15744

commit v3 on v2

--- a/solution.py
+++ b/solution.py
@@ -65,6 +65,7 @@
     raw_in,
     quat_rows,
     coeff_rows,
+    blocks,
     sent,
     got,
     tree,
@@ -143,8 +144,8 @@
     raw_copy = copies(raw_in.at[me], raw_in.at[me], raw_s, raw_r, vert_peer)
 
     pl.semaphore_wait(barrier, n_vert + n_col - 2)
+    each(n_col, lambda k: bas_copy(k).start())
     each(n_vert, lambda k: coeff_copy(k).start())
-    each(n_col, lambda k: bas_copy(k).start())
     each(n_vert, lambda k: index_copy(k).start())
     each(n_vert, lambda k: raw_copy(k).start())
 
@@ -203,16 +204,16 @@
     for i in range(n_vert):
         one = coeff_in[i].astype(F32)
         coeff_rows[i * SUB : (i + 1) * SUB, 0 : n_col * comps] = jnp.concatenate([one] * (SUB // own), axis=0)
-    blocks = [coeff_rows[:, kb * comps : (kb + 1) * comps].astype(BF16) for kb in range(n_col)]
-
-    each(n_col, lambda k: bas_copy(k).wait_recv())
+    for kb in range(n_col):
+        blocks[kb] = coeff_rows[:, kb * comps : (kb + 1) * comps].astype(BF16)
+
+    totals = [template[m : m + 1, :] + dot_nt(blocks[col], bas[col, m]) for m in range(3)]
+    for k in range(1, n_col):
+        bas_copy(k).wait_recv()
+        source = lax.rem(col + n_col - k, n_col)
+        totals = [totals[m] + dot_nt(blocks[source], bas[source, m]) for m in range(3)]
     r_axis = jnp.minimum((iota((rows, block), 0) % SUB) // own, 2)
-    full = jnp.zeros((rows, block), F32)
-    for m in range(3):
-        total = template[m : m + 1, :]
-        for kb in range(n_col):
-            total = total + dot_nt(blocks[kb], bas[kb, m])
-        full = jnp.where(r_axis == m, total, full)
+    full = jnp.where(r_axis == 0, totals[0], jnp.where(r_axis == 1, totals[1], totals[2]))
     share = dot_nt(full, regressor[...], EXACT)
     sent[:, 0, :, 0:block] = full.astype(BF16).astype(F32).reshape(n_vert, SUB, block)
     sent[:, 1, :, 0:joints] = share.reshape(n_vert, SUB, joints)
@@ -318,7 +319,7 @@
     dma = pltpu.SemaphoreType.DMA
     out = pl.pallas_call(
         functools.partial(kernel, n_vert, n_col),
-        out_shape=jax.ShapeDtypeStruct((3, own, n_vert * block), BF16),
+        out_shape=jax.ShapeDtypeStruct((3, own, n_vert * block), F32),
         in_specs=[anywhere] * 9,
         out_specs=vmem,
         scratch_shapes=[
@@ -333,6 +334,7 @@
             pltpu.VMEM((n_vert, slots, block), F32),
             pltpu.VMEM((SUB, LANES), F32),
             pltpu.VMEM((n_vert * SUB, total), F32),
+            pltpu.VMEM((n_col, n_vert * SUB, comps), BF16),
             pltpu.VMEM((n_vert, 2, SUB, LANES), F32),
             pltpu.VMEM((n_vert, 2, SUB, LANES), F32),
             pltpu.VMEM((joints, SUB, LANES), F32),
@@ -364,7 +366,7 @@
         jnp.transpose(skin_index),
         jnp.transpose(skin_raw),
     )
-    return jnp.transpose(out, (1, 0, 2))
+    return jnp.transpose(out, (1, 0, 2)).astype(BF16)
 
 
 def solution(mesh):

time: 17.9 us -> 17.9 us (level)
  other arithmetic: 0 us -> 1.33 us
  local copies, waits for them, and re-layouts: 1.31 us -> 0 us
    convert_element_type x0 -> x1, other arithmetic: none -> 1.33 us  [body(): return jnp.transpose(out, (1, 0, 2)).astype(BF16)]
    unnamed x1 -> x0, local copies, waits for them, and re-layouts: 1.31 us -> none
where the time goes in v3:
time: 17.9 us; the launch traced here: 17.7 us
  Pallas kernels  16.4 us (92%)
  other arithmetic  1.33 us (7%)
    pallas_call x1, Pallas kernels, body(): pl.pallas_call(functools.partial(kernel, n_vert, n_col), out_shape=jax.Sh...  16.4 us
    convert_element_type x1, other arithmetic, body(): return jnp.transpose(out, (1, 0, 2)).astype(BF16)  1.33 us

profile of v3, /device:TPU:0, one launch (start us, length us, event | category | flops | bytes accessed | tf_op | source)
XLA Modules:
  0.0 17.7 jit_solution(12581274786039726297)
XLA Ops:
  0.0 16.4 %shard_map.91 = f32[3,2,656]{2,1,0:T(2,128)} custom-call(s32[55]{0:T(128)} %parents_hbm.1, bf16[2,400]{1,0:T(2,128)(2,1)} %coeffs_hbm.1, bf16[3,82,100]{2,1,0:T(8,128)(2,1)} %bitcast.5, f32[3,82]{1,0:T(4,128)} %template_hbm.1, f32[55,82]{1,0:T(8,128)} %regressor_hbm.1, f32[2,4,55]{2,1,0:T(4,128)} %quat_hbm.1, f32[2,3]{1,0:T(2,128)} %shift_hbm.1, ...), custom_call_target="tpu_custom_call" | custom-call | tf_op jit(solution)/shard_map/pallas_call | solution.py:320
  16.4 1.3 %convert_bitcast_fusion = bf16[2,3,656]{2,0,1:T(2,128)(2,1)} fusion(f32[3,2,656]{2,1,0:T(2,128)} %shard_map.91), kind=kLoop, calls=%fused_computation | loop fusion | flops 3936 | bytes 23616 | tf_op jit(solution)/shard_map/convert_element_type | solution.py:369

commit v4 on v3

--- a/solution.py
+++ b/solution.py
@@ -145,7 +145,8 @@
 
     pl.semaphore_wait(barrier, n_vert + n_col - 2)
     each(n_col, lambda k: bas_copy(k).start())
-    each(n_vert, lambda k: coeff_copy(k).start())
+    lower = 1 - me // (n_vert // 2)
+    each(n_vert, lambda k: coeff_copy(k + lower * (n_vert - 2 * k)).start())
     each(n_vert, lambda k: index_copy(k).start())
     each(n_vert, lambda k: raw_copy(k).start())
 
@@ -229,7 +230,7 @@
             device_id_type=MESH,
         )
 
-    each(n_vert, lambda k: sent_copy(k).start())
+    each(n_vert, lambda k: sent_copy(k + lower * (n_vert - 2 * k)).start())
     got[me] = sent[me]
 
     each(n_vert, lambda k: index_copy(k).wait_recv())
@@ -319,7 +320,7 @@
     dma = pltpu.SemaphoreType.DMA
     out = pl.pallas_call(
         functools.partial(kernel, n_vert, n_col),
-        out_shape=jax.ShapeDtypeStruct((3, own, n_vert * block), F32),
+        out_shape=jax.ShapeDtypeStruct((3, own, n_vert * block), BF16),
         in_specs=[anywhere] * 9,
         out_specs=vmem,
         scratch_shapes=[
@@ -366,7 +367,7 @@
         jnp.transpose(skin_index),
         jnp.transpose(skin_raw),
     )
-    return jnp.transpose(out, (1, 0, 2)).astype(BF16)
+    return jnp.transpose(out, (1, 0, 2))
 
 
 def solution(mesh):

time: 17.9 us -> 17.8 us (level)
  other arithmetic: 1.33 us -> 0 us
  local copies, waits for them, and re-layouts: 0 us -> 1.31 us
    convert_element_type x1 -> x0, other arithmetic: 1.33 us -> none  [body(): return jnp.transpose(out, (1, 0, 2)).astype(BF16)]
    unnamed x0 -> x1, local copies, waits for them, and re-layouts: none -> 1.31 us
where the time goes in v4:
time: 17.8 us; the launch traced here: 17.6 us
  Pallas kernels  16.3 us (92%)
  local copies, waits for them, and re-layouts  1.31 us (7%)
    pallas_call x1, Pallas kernels, body(): pl.pallas_call(functools.partial(kernel, n_vert, n_col), out_shape=jax.Sh...  16.3 us
    unnamed x1, local copies, waits for them, and re-layouts  1.31 us

profile of v4, /device:TPU:0, one launch (start us, length us, event | category | flops | bytes accessed | tf_op | source)
XLA Modules:
  0.0 17.6 jit_solution(5564068067911720812)
XLA Ops:
  0.0 16.3 %shard_map.91 = bf16[3,2,656]{2,1,0:T(2,128)(2,1)} custom-call(s32[55]{0:T(128)} %parents_hbm.1, bf16[2,400]{1,0:T(2,128)(2,1)} %coeffs_hbm.1, bf16[3,82,100]{2,1,0:T(8,128)(2,1)} %bitcast.4, f32[3,82]{1,0:T(4,128)} %template_hbm.1, f32[55,82]{1,0:T(8,128)} %regressor_hbm.1, f32[2,4,55]{2,1,0:T(4,128)} %quat_hbm.1, f32[2,3]{1,0:T(2,128)} %shift_hbm.1, ...), custom_call_target="tpu_custom_call" | custom-call | tf_op jit(solution)/shard_map/pallas_call | solution.py:321
  16.3 1.3 %copy.11 = bf16[2,3,656]{2,0,1:T(2,128)(2,1)} copy(bf16[2,3,656]{2,0,1:T(2,128)(2,1)} %bitcast.5) | data formatting | bytes 15744
